TPU v7x, 256 devices: a whole 4x4x8 slice. The times are simulated.
256 devices in a mesh: img: 16 (over x, z_lo, core), patch: 16 (over y, z_hi).
Axes of the slice: x: 4, y: 4, z: 8 (z_hi: 4, z_lo: 2; z = z_hi * 2 + z_lo), core: 2. Of those that a mesh axis runs over, the one named last changes fastest.
Arguments:
- hidden: bfloat16 [32, 16, 128, 640], P('img', 'patch'), may hold values from -100 to 100
- stale_attn_in: bfloat16 [32, 16, 128, 640], P('img', 'patch'), may hold values from -100 to 100
- stale_conv_in: bfloat16 [32, 16, 128, 640], P('img', 'patch'), may hold values from -6 to 6
- ln_gain: float32 [640], replicated, may hold values from 0.25 to 1.75
- ln_bias: float32 [640], replicated, may hold values from -2 to 2
- w_qkv: bfloat16 [640, 1920], replicated, may hold values from -3 to 3
- w_out: bfloat16 [640, 640], replicated, may hold values from -0.25 to 0.25
- gn_gain: float32 [640], replicated, may hold values from 0.25 to 1.75
- gn_bias: float32 [640], replicated, may hold values from -1.5 to 1.5
- conv_weight: bfloat16 [3, 3, 640, 640], replicated, may hold values from -0.078125 to 0.078125
- conv_bias: float32 [640], replicated, may hold values from -1.5 to 1.5
- time_shift: float32 [32, 640], P('img'), may hold values from -6 to 6
Outputs:
- block_out: bfloat16 [32, 16, 128, 640], P('img', 'patch')
All inputs are finite; a program needn't handle non-finite values.
Results may differ from a plain program's by a relative error of at most 0.0075.
The roundings to bfloat16 on the way count: a program that leaves them out, or rounds other values in their place, can miss the bound.
Values may be sent and summed in bfloat16 or wider, within the bound.
No kernel may reach another device: no remote copies, remote signals or barrier semaphores. Data moves between devices by JAX's collectives and lax.ppermute only.
A program may use at most 128 MiB of HBM per device.

v0:
```python
import functools
import jax
import jax.numpy as jnp
from jax import lax
from jax.sharding import Mesh
from jax.sharding import PartitionSpec as P

GROUPS = 32
HEAD_DIM = 64
PATCH = ("patch_0", "patch_1")
EPSILON = 1e-05


def over_axes(shard, axes):
    return functools.reduce(lax.psum, axes, shard)


def extended(block, sides, width):
    for axis, dim in sides:
        count = lax.axis_size(axis)
        forward = [(i, i + 1) for i in range(count - 1)]
        backward = [(target, source) for source, target in forward]
        low = lax.ppermute(
            lax.slice_in_dim(block, block.shape[dim] - width, None, axis=dim), axis, forward
        )
        high = lax.ppermute(lax.slice_in_dim(block, 0, width, axis=dim), axis, backward)
        block = jnp.concatenate([low, block, high], axis=dim)
    return block


def layer_norm(values, gain, bias):
    values = values.astype(jnp.float32)
    centre = jnp.mean(values, -1, keepdims=True)
    centred = values - centre
    spread = jnp.mean(centred * centred, -1, keepdims=True)
    return (centred * lax.rsqrt(spread + EPSILON) * gain + bias).astype(jnp.bfloat16)


def absorb(softmax_state, queries, key_rows, value_rows, blocked):
    running_max, weight_sum, accum = softmax_state
    samples, key_count, channels = key_rows.shape
    head_count = channels // HEAD_DIM
    keys_split = key_rows.reshape(samples, key_count, head_count, HEAD_DIM)
    values_split = value_rows.reshape(samples, key_count, head_count, HEAD_DIM)
    scores = jnp.einsum(
        "sqhd,skhd->shqk", queries, keys_split, preferred_element_type=jnp.float32
    ) * HEAD_DIM ** (-0.5)
    scores = jnp.where(blocked[None, None, None, :], -jnp.inf, scores)
    new_max = jnp.maximum(running_max, jnp.max(scores, -1))
    rescale = jnp.exp(running_max - new_max)
    weights = jnp.exp(scores - new_max[..., None])
    weight_sum = weight_sum * rescale + jnp.sum(weights, -1)
    accum = accum * rescale[..., None] + jnp.einsum(
        "shqk,skhd->shqd",
        weights.astype(jnp.bfloat16),
        values_split,
        preferred_element_type=jnp.float32,
    )
    return (new_max, weight_sum, accum)


def shards(
    hidden,
    stale_attn_in,
    stale_conv_in,
    ln_gain,
    ln_bias,
    w_qkv,
    w_out,
    gn_gain,
    gn_bias,
    conv_weight,
    conv_bias,
    time_shift,
):
    samples, rows_dev, col_count, channels = hidden.shape
    head_count = channels // HEAD_DIM
    local_count = rows_dev * col_count
    own_start = lax.axis_index(PATCH) * local_count
    fresh_in = layer_norm(hidden, ln_gain, ln_bias).reshape(samples, local_count, channels)
    stale_in = layer_norm(stale_attn_in, ln_gain, ln_bias).reshape(samples, local_count, channels)
    fresh_qkv = jnp.einsum(
        "stc,cd->std", fresh_in, w_qkv, preferred_element_type=jnp.float32
    ).astype(jnp.bfloat16)
    queries = fresh_qkv[..., :channels].reshape(samples, local_count, head_count, HEAD_DIM)
    w_pair = w_qkv[:, channels:]
    initial = (
        jnp.full((samples, head_count, local_count), -jnp.inf, jnp.float32),
        jnp.zeros((samples, head_count, local_count), jnp.float32),
        jnp.zeros((samples, head_count, local_count, HEAD_DIM), jnp.float32),
    )
    no_block = jnp.zeros((local_count,), bool)
    softmax_state = absorb(
        initial,
        queries,
        fresh_qkv[..., channels : 2 * channels],
        fresh_qkv[..., 2 * channels :],
        no_block,
    )
    block_rows = lax.all_gather(stale_in, PATCH, axis=1, tiled=True)
    pair_rows = jnp.einsum(
        "snc,cd->snd", block_rows, w_pair, preferred_element_type=jnp.float32
    ).astype(jnp.bfloat16)
    positions = jnp.arange(block_rows.shape[1], dtype=jnp.int32)
    blocked = (positions >= own_start) & (positions < own_start + local_count)
    softmax_state = absorb(
        softmax_state, queries, pair_rows[..., :channels], pair_rows[..., channels:], blocked
    )
    running_max, weight_sum, accum = softmax_state
    attended = (
        (accum / weight_sum[..., None])
        .transpose(0, 2, 1, 3)
        .reshape(samples, local_count, channels)
        .astype(jnp.bfloat16)
    )
    attention_out = jnp.einsum("stc,cd->std", attended, w_out, preferred_element_type=jnp.float32)
    residual = (
        hidden.reshape(samples, local_count, channels).astype(jnp.float32) + attention_out
    ).astype(jnp.bfloat16)
    grouped = residual.astype(jnp.float32).reshape(samples, local_count, GROUPS, channels // GROUPS)
    cell_count = lax.axis_size(PATCH) * local_count * (channels // GROUPS)
    group_total, group_squares = (
        over_axes(jnp.sum(grouped, axis=(1, 3)), PATCH),
        over_axes(jnp.sum(grouped * grouped, axis=(1, 3)), PATCH),
    )
    group_mean = group_total / cell_count
    group_var = group_squares / cell_count - group_mean * group_mean
    centred = grouped - group_mean[:, None, :, None]
    normalized = (centred * lax.rsqrt(group_var + EPSILON)[:, None, :, None]).reshape(
        samples, local_count, channels
    )
    activated = (
        jax.nn.silu(normalized * gn_gain + gn_bias)
        .astype(jnp.bfloat16)
        .reshape(samples, rows_dev, col_count, channels)
    )
    stale_framed = extended(stale_conv_in, ((PATCH, 1),), 1)
    framed = jnp.concatenate([stale_framed[:, :1], activated, stale_framed[:, rows_dev + 1 :]], 1)
    framed = jnp.pad(framed, ((0, 0), (0, 0), (1, 1), (0, 0)))
    windows = [
        framed[:, tap_row : tap_row + rows_dev, tap_col : tap_col + col_count, :]
        for tap_row in range(3)
        for tap_col in range(3)
    ]
    unfolded = jnp.concatenate(windows, -1).reshape(samples * local_count, 9 * channels)
    convolved = jnp.dot(
        unfolded, conv_weight.reshape(9 * channels, channels), preferred_element_type=jnp.float32
    )
    summed_out = (
        convolved.reshape(samples, rows_dev, col_count, channels)
        + conv_bias
        + time_shift[:, None, None, :]
        + residual.astype(jnp.float32).reshape(samples, rows_dev, col_count, channels)
    )
    return summed_out.astype(jnp.bfloat16)


def solution(mesh):
    split = Mesh(mesh.devices.reshape(mesh.shape["img"], 4, 4), ("img", "patch_0", "patch_1"))
    return jax.shard_map(
        shards,
        mesh=split,
        in_specs=(
            P("img", PATCH, None, None),
            P("img", PATCH, None, None),
            P("img", PATCH, None, None),
            P(),
            P(),
            P(),
            P(),
            P(),
            P(),
            P(),
            P(),
            P("img", None),
        ),
        out_specs=P("img", PATCH, None, None),
        check_vma=False,
    )
```

profile of v0, /device:TPU:2, one launch (start us, length us, event | category | flops | bytes accessed | tf_op | source)
XLA Modules:
  0.0 191.6 jit_solution(10955897671697256372)
XLA Ops:
  6.5 1.2 convert_reduce_fusion.1
  7.7 1.2 fusion.54
  8.9 1.9 %fusion.57 = bf16[2,1,128,640]{3,2,0,1:T(8,128)(2,1)} fusion(bf16[2,1,128,640]{3,2,1,0:T(8,128)(2,1)} %param.13, f32[2,128]{1,0:T(2,128)S(1)} %add_rsqrt_fusion.1, f32[2,128]{1,0:T(2,128)S(1)} %broadcast_multiply_fusion.1, f32[640]{0:T(1024)} %param.16, f32[640]{0:T(1024)} %param.15), kind=kLoop, calls=%fused_computation.59 | loop fusion | flops 983040 | bytes 662528 | tf_op jit(solution)/shard_map/convert_element_type | solution.py:36
  10.9 0.0 all-gather.3.cloned.1.call-update
  10.9 1.3 collective-permute-start.1
  12.2 5.8 %collective-permute-start = (bf16[2,1,128,640]{3,2,0,1:T(8,128)(2,1)}, bf16[2,1,128,640]{3,2,0,1:T(8,128)(2,1)S(1)}, u32[]{:S(2)}, u32[]{:S(2)}) collective-permute-start(bf16[2,1,128,640]{3,2,0,1:T(8,128)(2,1)} %bitcast.118), channel_id=1, source_target_pairs={{0,1},{1,2},{2,3},{3,4},{4,5},{5,6},{6,7},{7,8},{8,9},{9,10},{10,1... | collective-permute-start | bytes 983048 | tf_op jit(solution)/shard_map/ppermute | solution.py:23
  18.0 1.1 convert_reduce_fusion
  19.1 1.2 fusion.50
  20.3 2.9 %convolution_convert_fusion.1 = bf16[2,128,1920]{2,1,0:T(8,128)(2,1)S(1)} fusion(bf16[640,1920]{1,0:T(8,128)(2,1)} %param.17, bf16[2,1,128,640]{3,2,1,0:T(8,128)(2,1)} %param.12, f32[640]{0:T(1024)} %param.16, f32[640]{0:T(1024)} %param.15, f32[2,128]{1,0:T(2,128)S(1)} %add_rsqrt_fusion.2, f32[2,128]{1,0:T(2,128)S(1)} %broadcast_multiply_fusion.2), kind=kOutput, calls=%fused_computation.13 | convolution fusion | flops 630620160 | bytes 3775488 | tf_op jit(solution)/shard_map/stc,cd->std/dot_general | solution.py:82
  23.3 0.1 fusion.78
  23.4 0.2 copy.27
  23.6 0.2 copy.28
  23.8 0.9 copy.29
  24.7 0.4 fusion.79
  25.1 0.2 fusion.41
  25.3 75.6 %all-gather.3.cloned.1.call-done = bf16[2,1,2048,640]{3,2,0,1:T(8,128)(2,1)} async-done(((bf16[2,1,128,640]{3,2,0,1:T(8,128)(2,1)}), bf16[2,1,2048,640]{3,2,0,1:T(8,128)(2,1)}) %all-gather.3.cloned.1.call-update) | async-done | bytes 5242896 | tf_op jit(solution)/shard_map/all_gather | solution.py:100
  101.0 13.2 %convolution_convert_fusion = bf16[2,2048,1280]{1,2,0:T(8,128)(2,1)} fusion(bf16[2,1,2048,640]{3,2,0,1:T(8,128)(2,1)} %all-gather.3.cloned.1.call-done, bf16[640,1920]{1,0:T(8,128)(2,1)} %param.17), kind=kOutput, calls=%fused_computation.5 | convolution fusion | flops 6716129280 | bytes 17367040 | tf_op jit(solution)/shard_map/snc,cd->snd/dot_general | solution.py:101
  114.2 10.2 %fusion.77 = (bf16[2,2048,640]{1,2,0:T(8,128)(2,1)}, bf16[2,2048,640]{1,2,0:T(8,128)(2,1)}) fusion(bf16[2,2048,1280]{1,2,0:T(8,128)(2,1)} %convolution_convert_fusion), kind=kLoop, calls=%fused_computation.99 | loop fusion | bytes 20971520 | tf_op jit(solution)/shard_map/slice | solution.py:107
  124.4 5.1 %fusion = (f32[2,10,128]{2,1,0:T(8,128)S(1)}, f32[2,10,128,2048]{3,2,1,0:T(8,128)S(1)}) fusion(pred[2048]{0:T(1024)(128)(4,1)S(1)} %fusion.72, bf16[2,128,10,64]{1,3,2,0:T(8,128)(2,1)S(1)} %bitcast.112, bf16[2,2048,10,64]{1,3,2,0:T(8,128)(2,1)} %bitcast.109), kind=kOutput, calls=%fused_computation.2 | convolution fusion | flops 686814720 | bytes 26554368 | tf_op jit(solution)/shard_map/sqhd,skhd->shqk/dot_general | solution.py:45
  129.5 4.7 %fusion.1 = f32[2,10,128]{2,1,0:T(8,128)S(1)} fusion(f32[2,10,128,2048]{3,2,1,0:T(8,128)S(1)} %get-tuple-element.24, f32[2,10,128]{2,1,0:T(8,128)S(1)} %max.18, pred[2048]{0:T(1024)(128)(4,1)S(1)} %fusion.72), kind=kLoop, calls=%fused_computation.3 | loop fusion | flops 20968960 | bytes 20994048 | tf_op jit(solution)/shard_map/reduce_sum | solution.py:52
  134.2 2.3 %copy-done.1 = f32[2,10,128,2048]{3,2,1,0:T(8,128)} copy-done((f32[2,10,128,2048]{3,2,1,0:T(8,128)}, f32[2,10,128,2048]{3,2,1,0:T(8,128)S(1)}, u32[]{:S(2)}) %copy-start.1) | copy-done | bytes 20971544
  136.5 10.8 %fusion.17 = f32[2,128,10,64]{1,3,2,0:T(8,128)S(1)} fusion(bf16[2,2048,10,64]{1,3,2,0:T(8,128)(2,1)} %bitcast.110, f32[2,10,128,2048]{3,2,1,0:T(8,128)} %copy-done.1, f32[2,10,128]{2,1,0:T(8,128)S(1)} %max.18, pred[2048]{0:T(1024)(128)(4,1)S(1)} %fusion.72), kind=kOutput, calls=%fused_computation.26 | convolution fusion | flops 692060160 | bytes 26882048 | tf_op jit(solution)/shard_map/shqk,skhd->shqd/dot_general | solution.py:53
  147.3 0.0 copy-start.2
  147.4 0.0 copy-start.4
  147.4 0.0 copy-start.5
  147.4 0.3 fusion.31
  147.8 0.5 copy-done.2
  148.3 0.5 fusion.75
  148.8 0.1 reduce_sum.102
  148.9 0.1 reduce_sum.99
  149.1 0.1 reduce_sum.103
  149.1 0.1 reduce_sum.100
  149.2 10.2 %all-reduce.2 = (f32[2,32]{1,0:T(2,128)S(1)}, f32[2,32]{1,0:T(2,128)S(1)}) all-reduce(f32[2,32]{1,0:T(2,128)S(1)} %reduce_sum.103, f32[2,32]{1,0:T(2,128)S(1)} %reduce_sum.100), channel_id=1, replica_groups=mesh['img'=16,'patch_0'=4,'patch_1'=4] {'patch_0'}, use_global_device_ids=true, to_apply=%region_14.15 | all-reduce | flops 128 | bytes 1024 | tf_op jit(solution)/shard_map/psum | solution.py:15
  159.4 17.1 %all-reduce.1 = (f32[2,32]{1,0:T(2,128)S(1)}, f32[2,32]{1,0:T(2,128)S(1)}) all-reduce(f32[2,32]{1,0:T(2,128)S(1)} %get-tuple-element.9, f32[2,32]{1,0:T(2,128)S(1)} %get-tuple-element.10), channel_id=1, replica_groups=mesh['img'=16,'patch_0'=4,'patch_1'=4] {'patch_1'}, use_global_device_ids=true, to_apply=%region_15.16 | all-reduce | flops 128 | bytes 1024 | tf_op jit(solution)/shard_map/psum | solution.py:15
  176.6 0.1 mul.129
  176.7 0.1 mul.130
  176.8 0.1 sub.82
  176.9 0.1 sub.83
  177.0 0.2 fusion.67
  177.2 0.0 collective-permute-done
  177.2 0.3 fusion.44
  177.6 0.0 copy-start.6
  177.6 0.0 copy-start.7
  177.6 0.1 slice_dynamic-update-slice_fusion.4
  177.8 0.3 constant_dynamic-update-slice_fusion.1
  178.0 0.1 slice_dynamic-update-slice_fusion.2
  178.2 0.1 slice_dynamic-update-slice_fusion
  178.4 6.4 %fusion.38 = bf16[2,1,128,640]{3,2,1,0:T(8,128)(2,1)} fusion(f32[2,128,640]{2,1,0:T(8,128)S(1)} %get-tuple-element.25, bf16[5760,640,1]{1,0,2:T(8,128)(2,1)} %bitcast.116, bf16[2,1,128,5760]{3,2,0,1:T(8,128)(2,1)S(1)} %slice_dynamic-update-slice_fusion, f32[2,640]{1,0:T(2,128)S(1)} %copy-done.6, f32[640]{0:T(1024)S(1)} %copy-done.7), kind=kOutput, calls=%fused_computation.37 | convolution fusion | flops 1888092160 | bytes 11312640 | tf_op jit(solution)/shard_map/dot_general | solution.py:146
  (24 shorter events, 0.3 us)
Async XLA Ops:
  6.5 141.2 %copy-start = (bf16[640,640]{1,0:T(8,128)(2,1)S(1)}, bf16[640,640]{1,0:T(8,128)(2,1)}, u32[]{:S(2)}) copy-start(bf16[640,640]{1,0:T(8,128)(2,1)} %param.18) | copy-start | bytes 2457604
  6.5 94.4 %all-gather.3.cloned.1.call-start = ((), (), s32[]{:S(2)}) async-start(), calls=%async_computation | async-start | bytes 5570560 | tf_op jit(solution)/shard_map/all_gather | solution.py:100
  10.9 166.3 %collective-permute-start.1 = (bf16[2,1,128,640]{3,2,0,1:T(8,128)(2,1)}, bf16[2,1,128,640]{3,2,0,1:T(8,128)(2,1)S(1)}, u32[]{:S(2)}, u32[]{:S(2)}) collective-permute-start(bf16[2,1,128,640]{3,2,0,1:T(8,128)(2,1)} %bitcast.117), channel_id=1, source_target_pairs={{1,0},{2,1},{3,2},{4,3},{5,4},{6,5},{7,6},{8,7},{9,8},{10,9},{11,1... | collective-permute-start | bytes 983048 | tf_op jit(solution)/shard_map/ppermute | solution.py:26
  12.2 165.0 %collective-permute-start = (bf16[2,1,128,640]{3,2,0,1:T(8,128)(2,1)}, bf16[2,1,128,640]{3,2,0,1:T(8,128)(2,1)S(1)}, u32[]{:S(2)}, u32[]{:S(2)}) collective-permute-start(bf16[2,1,128,640]{3,2,0,1:T(8,128)(2,1)} %bitcast.118), channel_id=1, source_target_pairs={{0,1},{1,2},{2,3},{3,4},{4,5},{5,6},{6,7},{7,8},{8,9},{9,10},{10,1... | collective-permute-start | bytes 983048 | tf_op jit(solution)/shard_map/ppermute | solution.py:23
  129.5 7.0 %copy-start.1 = (f32[2,10,128,2048]{3,2,1,0:T(8,128)}, f32[2,10,128,2048]{3,2,1,0:T(8,128)S(1)}, u32[]{:S(2)}) copy-start(f32[2,10,128,2048]{3,2,1,0:T(8,128)S(1)} %get-tuple-element.24) | copy-start | bytes 62914564
  136.5 10.9 %copy-start.3 = (bf16[2,128,640]{1,2,0:T(8,128)(2,1)S(1)}, bf16[2,128,640]{1,2,0:T(8,128)(2,1)}, u32[]{:S(2)}) copy-start(bf16[2,128,640]{1,2,0:T(8,128)(2,1)} %copy.29) | copy-start | bytes 983044
  147.3 1.0 copy-start.2
  147.4 29.6 %copy-start.4 = (f32[640]{0:T(1024)S(1)}, f32[640]{0:T(1024)}, u32[]{:S(2)}) copy-start(f32[640]{0:T(1024)} %param.20) | copy-start | bytes 7684
  147.4 29.6 %copy-start.5 = (f32[640]{0:T(1024)S(1)}, f32[640]{0:T(1024)}, u32[]{:S(2)}) copy-start(f32[640]{0:T(1024)} %param.19) | copy-start | bytes 7684
  177.6 0.8 copy-start.6
  177.6 0.8 copy-start.7
Sparse Core Ops, SparseCore 0:
  11.0 89.9 all-gather.2
where the time goes:
time: 192 us
  waiting for transfers between devices  75.7 us (39%)
  matrix products  39.7 us (21%)
  blocking collectives  27.3 us (14%)
  local copies, waits for them, and re-layouts  15.5 us (8%)
  between operations  13.7 us (7%)
  other arithmetic  12.5 us (7%)
  starting transfers between devices  7.12 us (4%)
    all_gather x1, waiting for transfers between devices, shards(): block_rows = lax.all_gather(stale_in, PATCH, axis=1, tiled=True)  75.6 us
    psum x2, blocking collectives, over_axes(): return functools.reduce(lax.psum, axes, shard)  27.3 us
    dot_general x1, matrix products, shards(): jnp.einsum('snc,cd->snd', block_rows, w_pair, preferred_element_type=jnp....  13.2 us
    dot_general x2, matrix products, absorb(): jnp.einsum('shqk,skhd->shqd', weights.astype(jnp.bfloat16), values_split,...  11.2 us
    slice x1, local copies, waits for them, and re-layouts, shards(): pair_rows[..., :channels]  10.2 us
    dot_general x1, matrix products, shards(): jnp.dot(unfolded, conv_weight.reshape(9 * channels, channels), preferred_...  6.36 us
    ppermute x1, starting transfers between devices, extended(): lax.ppermute(lax.slice_in_dim(block, block.shape[dim] - width, None, axis...  5.83 us
    dot_general x2, matrix products, absorb(): jnp.einsum('sqhd,skhd->shqk', queries, keys_split, preferred_element_type...  5.51 us
  transfers between devices with their start and end apart: 3, of which 1 were waited for; matrix products, arithmetic and copies ran while one was open for 28% of the time, Pallas kernels for 0%

commit v1 on v0

--- a/solution.py
+++ b/solution.py
@@ -97,7 +97,9 @@
         fresh_qkv[..., 2 * channels :],
         no_block,
     )
-    block_rows = lax.all_gather(stale_in, PATCH, axis=1, tiled=True)
+    block_rows = jnp.concatenate(
+        lax.all_to_all(jnp.stack([stale_in] * lax.axis_size(PATCH)), PATCH, 0, 0), axis=1
+    )
     pair_rows = jnp.einsum(
         "snc,cd->snd", block_rows, w_pair, preferred_element_type=jnp.float32
     ).astype(jnp.bfloat16)

time: 192 us -> 225 us (1.17); the launches traced: 192 us -> 222 us
  waiting for transfers between devices: 75.7 us -> 107 us
  between operations: 13.7 us -> 0.37 us
  starting transfers between devices: 7.12 us -> 18.1 us
  local copies, waits for them, and re-layouts: 15.5 us -> 22 us
  other arithmetic: 12.5 us -> 9.79 us
    all_to_all x0 -> x1, waiting for transfers between devices: none -> 107 us  [shards(): lax.all_to_all(jnp.stack([stale_in] * lax.axis_size(PATCH)), PATCH, 0, 0)]
    all_gather x1 -> x0, waiting for transfers between devices: 75.6 us -> none  [shards(): block_rows = lax.all_gather(stale_in, PATCH, axis=1, tiled=True)]
    all_to_all x0 -> x1, starting transfers between devices: none -> 11.4 us  [shards(): lax.all_to_all(jnp.stack([stale_in] * lax.axis_size(PATCH)), PATCH, 0, 0)]
    reshape x0 -> x1, local copies, waits for them, and re-layouts: none -> 3.26 us  [shards(): jnp.concatenate(lax.all_to_all(jnp.stack([stale_in] * lax.axis_size(PATCH...]
    another operation x0 -> x1, local copies, waits for them, and re-layouts: none -> 3.06 us  [shards(): jnp.stack([stale_in] * lax.axis_size(PATCH))]
  transfers between devices with their start and end apart: 3 -> 3, of which waited for: 1 -> 1; matrix products, arithmetic and copies ran while one was open for 28% -> 24% of each run, Pallas kernels for 0% -> 0%
where the time goes in v1:
time: 225 us; the launch traced here: 222 us
  waiting for transfers between devices  107 us (48%)
  matrix products  38.6 us (17%)
  blocking collectives  25.5 us (11%)
  local copies, waits for them, and re-layouts  22 us (10%)
  starting transfers between devices  18.1 us (8%)
  other arithmetic  9.79 us (4%)
    all_to_all x1, waiting for transfers between devices, shards(): lax.all_to_all(jnp.stack([stale_in] * lax.axis_size(PATCH)), PATCH, 0, 0)  107 us
    psum x2, blocking collectives, over_axes(): return functools.reduce(lax.psum, axes, shard)  25.5 us
    all_to_all x1, starting transfers between devices, shards(): lax.all_to_all(jnp.stack([stale_in] * lax.axis_size(PATCH)), PATCH, 0, 0)  11.4 us
    dot_general x1, matrix products, shards(): jnp.einsum('snc,cd->snd', block_rows, w_pair, preferred_element_type=jnp....  11.3 us
    dot_general x2, matrix products, absorb(): jnp.einsum('shqk,skhd->shqd', weights.astype(jnp.bfloat16), values_split,...  11.2 us
    slice x1, local copies, waits for them, and re-layouts, shards(): pair_rows[..., :channels]  10.2 us
    dot_general x2, matrix products, absorb(): jnp.einsum('sqhd,skhd->shqk', queries, keys_split, preferred_element_type...  6.48 us
    dot_general x1, matrix products, shards(): jnp.dot(unfolded, conv_weight.reshape(9 * channels, channels), preferred_...  6.36 us
  transfers between devices with their start and end apart: 3, of which 1 were waited for; matrix products, arithmetic and copies ran while one was open for 24% of the time, Pallas kernels for 0%

profile of v1, /device:TPU:2, one launch (start us, length us, event | category | flops | bytes accessed | tf_op | source)
XLA Modules:
  0.0 221.6 jit_solution(6152872311339758886)
XLA Ops:
  0.0 1.2 convert_reduce_fusion.1
  1.2 1.2 fusion.53
  2.4 1.2 fusion.59
  3.6 3.1 %stack.3 = bf16[16,2,128,640]{3,2,1,0:T(8,128)(2,1)} broadcast(bf16[2,128,640]{2,1,0:T(8,128)(2,1)S(1)} %fusion.59), dimensions={1,2,3} | broadcast | bytes 5570560 | tf_op jit(solution)/shard_map/stack | solution.py:101
  6.7 11.4 %all-to-all-start = ((bf16[16,2,128,640]{3,2,1,0:T(8,128)(2,1)}), bf16[16,2,128,640]{3,2,1,0:T(8,128)(2,1)}, u32[]{:S(2)}, u32[]{:S(2)}) async-start(bf16[16,2,128,640]{3,2,1,0:T(8,128)(2,1)} %stack.3), calls=%async_computation | async-start | bytes 10485760 | tf_op jit(solution)/shard_map/all_to_all | solution.py:101
  18.1 1.3 collective-permute-start.1
  19.4 5.5 %collective-permute-start = (bf16[2,1,128,640]{3,2,0,1:T(8,128)(2,1)}, bf16[2,1,128,640]{3,2,0,1:T(8,128)(2,1)S(1)}, u32[]{:S(2)}, u32[]{:S(2)}) collective-permute-start(bf16[2,1,128,640]{3,2,0,1:T(8,128)(2,1)} %bitcast), channel_id=1, source_target_pairs={{0,1},{1,2},{2,3},{3,4},{4,5},{5,6},{6,7},{7,8},{8,9},{9,10},{10,1... | collective-permute-start | bytes 983048 | tf_op jit(solution)/shard_map/ppermute | solution.py:23
  24.9 0.1 convert_reduce_fusion
  25.0 0.2 fusion.49
  25.2 2.8 %convolution_convert_fusion.1 = bf16[2,128,1920]{2,1,0:T(8,128)(2,1)S(1)} fusion(bf16[640,1920]{1,0:T(8,128)(2,1)} %param.17, bf16[2,1,128,640]{3,2,1,0:T(8,128)(2,1)S(1)} %copy-done.2, f32[640]{0:T(1024)S(1)} %copy-done.6, f32[640]{0:T(1024)S(1)} %copy-done.7, f32[2,128]{1,0:T(2,128)S(1)} %add_rsqrt_fusion.2, f32[2,128]{1,0:T(2,128)S(1)} %broadcast_multiply_fusion.2), kind=kOutput, calls=%fused_computation.12 | convolution fusion | flops 630620160 | bytes 3775488 | tf_op jit(solution)/shard_map/stc,cd->std/dot_general | solution.py:82
  28.0 0.1 fusion.78
  28.1 0.2 copy.38
  28.3 0.9 copy.39
  29.2 0.9 copy.40
  30.1 1.4 fusion.79
  31.5 0.2 fusion.40
  31.7 107.1 %all-to-all-done = bf16[16,2,128,640]{3,2,1,0:T(8,128)(2,1)} async-done(((bf16[16,2,128,640]{3,2,1,0:T(8,128)(2,1)}), bf16[16,2,128,640]{3,2,1,0:T(8,128)(2,1)}, u32[]{:S(2)}, u32[]{:S(2)}) %all-to-all-start) | async-done | bytes 5242912 | tf_op jit(solution)/shard_map/all_to_all | solution.py:101
  138.9 3.3 %copy.43 = bf16[2,16,128,640]{3,2,1,0:T(8,128)(2,1)S(1)} copy(bf16[2,16,128,640]{3,2,0,1:T(8,128)(2,1)} %bitcast.12) | data formatting | bytes 10485760 | tf_op jit(solution)/shard_map/reshape | solution.py:100
  142.2 11.3 %convolution_convert_fusion = bf16[2,2048,1280]{1,2,0:T(8,128)(2,1)} fusion(bf16[2,2048,640]{2,1,0:T(8,128)(2,1)S(1)} %bitcast.113, bf16[640,1920]{1,0:T(8,128)(2,1)S(1)} %copy-done.8), kind=kOutput, calls=%fused_computation.5 | convolution fusion | flops 6716129280 | bytes 17367040 | tf_op jit(solution)/shard_map/snc,cd->snd/dot_general | solution.py:103
  153.4 10.2 %fusion.77 = (bf16[2,2048,640]{1,2,0:T(8,128)(2,1)}, bf16[2,2048,640]{1,2,0:T(8,128)(2,1)}) fusion(bf16[2,2048,1280]{1,2,0:T(8,128)(2,1)} %convolution_convert_fusion), kind=kLoop, calls=%fused_computation.99 | loop fusion | bytes 20971520 | tf_op jit(solution)/shard_map/slice | solution.py:109
  163.6 5.1 %fusion = (f32[2,10,128]{2,1,0:T(8,128)S(1)}, f32[2,10,128,2048]{3,2,1,0:T(8,128)S(1)}) fusion(pred[2048]{0:T(1024)(128)(4,1)S(1)} %fusion.72, bf16[2,128,10,64]{1,3,2,0:T(8,128)(2,1)S(1)} %bitcast.115, bf16[2,2048,10,64]{1,3,2,0:T(8,128)(2,1)} %bitcast.111), kind=kOutput, calls=%fused_computation.2 | convolution fusion | flops 686814720 | bytes 26554368 | tf_op jit(solution)/shard_map/sqhd,skhd->shqk/dot_general | solution.py:45
  168.7 4.7 %fusion.1 = f32[2,10,128]{2,1,0:T(8,128)S(1)} fusion(f32[2,10,128,2048]{3,2,1,0:T(8,128)S(1)} %get-tuple-element.24, f32[2,10,128]{2,1,0:T(8,128)S(1)} %max.18, pred[2048]{0:T(1024)(128)(4,1)S(1)} %fusion.72), kind=kLoop, calls=%fused_computation.3 | loop fusion | flops 20968960 | bytes 20994048 | tf_op jit(solution)/shard_map/reduce_sum | solution.py:52
  173.4 2.3 %copy-done.1 = f32[2,10,128,2048]{3,2,1,0:T(8,128)} copy-done((f32[2,10,128,2048]{3,2,1,0:T(8,128)}, f32[2,10,128,2048]{3,2,1,0:T(8,128)S(1)}, u32[]{:S(2)}) %copy-start.1) | copy-done | bytes 20971544
  175.7 10.8 %fusion.16 = f32[2,128,10,64]{1,3,2,0:T(8,128)S(1)} fusion(bf16[2,2048,10,64]{1,3,2,0:T(8,128)(2,1)} %bitcast.112, f32[2,10,128,2048]{3,2,1,0:T(8,128)} %copy-done.1, f32[2,10,128]{2,1,0:T(8,128)S(1)} %max.18, pred[2048]{0:T(1024)(128)(4,1)S(1)} %fusion.72), kind=kOutput, calls=%fused_computation.25 | convolution fusion | flops 692060160 | bytes 26882048 | tf_op jit(solution)/shard_map/shqk,skhd->shqd/dot_general | solution.py:53
  186.6 0.0 copy-start.4
  186.6 0.0 copy-start.5
  186.6 0.3 fusion.30
  187.0 0.5 fusion.75
  187.5 0.1 reduce_sum.102
  187.6 0.1 reduce_sum.99
  187.7 0.1 reduce_sum.103
  187.8 0.1 reduce_sum.100
  187.9 16.7 %all-reduce.2 = (f32[2,32]{1,0:T(2,128)S(1)}, f32[2,32]{1,0:T(2,128)S(1)}) all-reduce(f32[2,32]{1,0:T(2,128)S(1)} %reduce_sum.103, f32[2,32]{1,0:T(2,128)S(1)} %reduce_sum.100), channel_id=1, replica_groups=mesh['img'=16,'patch_0'=4,'patch_1'=4] {'patch_0'}, use_global_device_ids=true, to_apply=%region_14.15 | all-reduce | flops 128 | bytes 1024 | tf_op jit(solution)/shard_map/psum | solution.py:15
  204.6 8.8 %all-reduce.1 = (f32[2,32]{1,0:T(2,128)S(1)}, f32[2,32]{1,0:T(2,128)S(1)}) all-reduce(f32[2,32]{1,0:T(2,128)S(1)} %get-tuple-element.9, f32[2,32]{1,0:T(2,128)S(1)} %get-tuple-element.10), channel_id=1, replica_groups=mesh['img'=16,'patch_0'=4,'patch_1'=4] {'patch_1'}, use_global_device_ids=true, to_apply=%region_15.16 | all-reduce | flops 128 | bytes 1024 | tf_op jit(solution)/shard_map/psum | solution.py:15
  213.4 0.1 mul.129
  213.5 0.1 mul.130
  213.6 0.1 sub.82
  213.7 0.1 sub.83
  213.8 0.2 fusion.67
  214.1 0.0 collective-permute-done.1
  214.1 0.3 fusion.43
  214.4 0.0 copy-start.9
  214.4 0.0 copy-start.10
  214.5 0.1 slice_dynamic-update-slice_fusion.4
  214.6 0.3 constant_dynamic-update-slice_fusion.1
  214.9 0.1 slice_dynamic-update-slice_fusion.2
  215.1 0.1 slice_dynamic-update-slice_fusion
  215.2 6.4 %fusion.37 = bf16[2,1,128,640]{3,2,1,0:T(8,128)(2,1)} fusion(f32[2,128,640]{2,1,0:T(8,128)S(1)} %get-tuple-element.25, bf16[5760,640,1]{1,0,2:T(8,128)(2,1)} %bitcast.119, bf16[2,1,128,5760]{3,2,0,1:T(8,128)(2,1)S(1)} %slice_dynamic-update-slice_fusion, f32[2,640]{1,0:T(2,128)S(1)} %copy-done.9, f32[640]{0:T(1024)S(1)} %copy-done.10), kind=kOutput, calls=%fused_computation.36 | convolution fusion | flops 1888092160 | bytes 11312640 | tf_op jit(solution)/shard_map/dot_general | solution.py:148
  (31 shorter events, 0.3 us)
Async XLA Ops:
  0.0 187.0 %copy-start = (bf16[640,640]{1,0:T(8,128)(2,1)S(1)}, bf16[640,640]{1,0:T(8,128)(2,1)}, u32[]{:S(2)}) copy-start(bf16[640,640]{1,0:T(8,128)(2,1)} %param.18) | copy-start | bytes 2457604
  6.7 18.2 %copy-start.2 = (bf16[2,1,128,640]{3,2,1,0:T(8,128)(2,1)S(1)}, bf16[2,1,128,640]{3,2,1,0:T(8,128)(2,1)}, u32[]{:S(2)}) copy-start(bf16[2,1,128,640]{3,2,1,0:T(8,128)(2,1)} %param.12) | copy-start | bytes 983044
  6.7 18.6 %copy-start.6 = (f32[640]{0:T(1024)S(1)}, f32[640]{0:T(1024)}, u32[]{:S(2)}) copy-start(f32[640]{0:T(1024)} %param.16) | copy-start | bytes 7684
  6.7 18.6 %copy-start.7 = (f32[640]{0:T(1024)S(1)}, f32[640]{0:T(1024)}, u32[]{:S(2)}) copy-start(f32[640]{0:T(1024)} %param.15) | copy-start | bytes 7684
  6.7 132.2 %all-to-all-start = ((bf16[16,2,128,640]{3,2,1,0:T(8,128)(2,1)}), bf16[16,2,128,640]{3,2,1,0:T(8,128)(2,1)}, u32[]{:S(2)}, u32[]{:S(2)}) async-start(bf16[16,2,128,640]{3,2,1,0:T(8,128)(2,1)} %stack.3), calls=%async_computation | async-start | bytes 10485760 | tf_op jit(solution)/shard_map/all_to_all | solution.py:101
  18.1 196.0 %collective-permute-start.1 = (bf16[2,1,128,640]{3,2,0,1:T(8,128)(2,1)}, bf16[2,1,128,640]{3,2,0,1:T(8,128)(2,1)S(1)}, u32[]{:S(2)}, u32[]{:S(2)}) collective-permute-start(bf16[2,1,128,640]{3,2,0,1:T(8,128)(2,1)} %bitcast), channel_id=1, source_target_pairs={{1,0},{2,1},{3,2},{4,3},{5,4},{6,5},{7,6},{8,7},{9,8},{10,9},{11,1... | collective-permute-start | bytes 983048 | tf_op jit(solution)/shard_map/ppermute | solution.py:26
  19.4 194.7 %collective-permute-start = (bf16[2,1,128,640]{3,2,0,1:T(8,128)(2,1)}, bf16[2,1,128,640]{3,2,0,1:T(8,128)(2,1)S(1)}, u32[]{:S(2)}, u32[]{:S(2)}) collective-permute-start(bf16[2,1,128,640]{3,2,0,1:T(8,128)(2,1)} %bitcast), channel_id=1, source_target_pairs={{0,1},{1,2},{2,3},{3,4},{4,5},{5,6},{6,7},{7,8},{8,9},{9,10},{10,1... | collective-permute-start | bytes 983048 | tf_op jit(solution)/shard_map/ppermute | solution.py:23
  138.9 3.3 %copy-start.8 = (bf16[640,1920]{1,0:T(8,128)(2,1)S(1)}, bf16[640,1920]{1,0:T(8,128)(2,1)}, u32[]{:S(2)}) copy-start(bf16[640,1920]{1,0:T(8,128)(2,1)} %param.17) | copy-start | bytes 7372804
  168.7 7.0 %copy-start.1 = (f32[2,10,128,2048]{3,2,1,0:T(8,128)}, f32[2,10,128,2048]{3,2,1,0:T(8,128)S(1)}, u32[]{:S(2)}) copy-start(f32[2,10,128,2048]{3,2,1,0:T(8,128)S(1)} %get-tuple-element.24) | copy-start | bytes 62914564
  175.7 10.9 %copy-start.3 = (bf16[2,128,640]{1,2,0:T(8,128)(2,1)S(1)}, bf16[2,128,640]{1,2,0:T(8,128)(2,1)}, u32[]{:S(2)}) copy-start(bf16[2,128,640]{1,2,0:T(8,128)(2,1)} %copy.40) | copy-start | bytes 983044
  186.6 27.2 %copy-start.4 = (f32[640]{0:T(1024)S(1)}, f32[640]{0:T(1024)}, u32[]{:S(2)}) copy-start(f32[640]{0:T(1024)} %param.20) | copy-start | bytes 7684
  186.6 27.2 %copy-start.5 = (f32[640]{0:T(1024)S(1)}, f32[640]{0:T(1024)}, u32[]{:S(2)}) copy-start(f32[640]{0:T(1024)} %param.19) | copy-start | bytes 7684
  214.4 0.8 copy-start.9
  214.4 0.8 copy-start.10
